TPU v7x, 32 devices: a whole 2x2x4 slice. The times are simulated.
32 devices in a mesh: dp: 4 (over x, y), sp: 8 (over z, core).
Axes of the slice: x: 2, y: 2, z: 4, core: 2. Of those that a mesh axis runs over, the one named last changes fastest.
Arguments:
- x_special: bfloat16 [64, 1, 1024], P('dp'), parts along dimension 0
- x_patch: bfloat16 [64, 512, 1024], P('dp', 'sp'), parts along dimension 0
- dy_special: bfloat16 [64, 1, 1024], P('dp'), parts along dimension 0
- dy_patch: bfloat16 [64, 512, 1024], P('dp', 'sp'), parts along dimension 0
- ln_scale: float32 [1024], replicated
- ln_bias: float32 [1024], replicated
- w_qkv: bfloat16 [1024, 3072], replicated
- b_qkv: float32 [3072], replicated
- w_proj: bfloat16 [1024, 1024], replicated
- b_proj: float32 [1024], replicated
- layer_scale: float32 [1024], replicated
Outputs:
- output 1: bfloat16 [64, 1, 1024], P('dp'), parts along dimension 0
- output 2: bfloat16 [64, 512, 1024], P('dp', 'sp'), parts along dimension 0
- output 3: bfloat16 [64, 1, 1024], P('dp'), parts along dimension 0
- output 4: bfloat16 [64, 512, 1024], P('dp', 'sp'), parts along dimension 0
- output 5: float32 [4096], P('dp'), parts along dimension 0
- output 6: float32 [4096], P('dp'), parts along dimension 0
- output 7: float32 [4096, 3072], P('dp'), parts along dimension 0
- output 8: float32 [12288], P('dp'), parts along dimension 0
- output 9: float32 [4096, 1024], P('dp'), parts along dimension 0
- output 10: float32 [4096], P('dp'), parts along dimension 0
- output 11: float32 [4096], P('dp'), parts along dimension 0
There are 4 independent parts. A program takes and returns all parts, laid end to end along the dimension named above; an argument that names none is the same for every part.
All inputs are finite; a program needn't handle non-finite values.
Results may differ from a plain program's by a relative error of at most 0.01016.
Values are sent between devices in bfloat16 or wider.
A program may use at most 1 GiB of HBM per device.

v0:
```python
import jax
import jax.numpy as jnp
from jax import lax
from jax.sharding import PartitionSpec as P

HEAD_DIM = 64
LN_EPS = 1e-6
ATTN_SCALE = HEAD_DIM ** -0.5


def norm_forward(x_rows, ln_scale, ln_bias):
    x_float = x_rows.astype(jnp.float32)
    centered = x_float - jnp.mean(x_float, axis=-1, keepdims=True)
    inv_std = lax.rsqrt(jnp.mean(centered * centered, axis=-1, keepdims=True) + LN_EPS)
    x_hat = centered * inv_std
    return (x_hat * ln_scale + ln_bias).astype(jnp.bfloat16), x_hat, inv_std


def norm_backward(d_normed, x_hat, inv_std, ln_scale):
    grad_float = d_normed.astype(jnp.float32)
    grad_hat = grad_float * ln_scale
    d_row_vals = inv_std * (grad_hat - jnp.mean(grad_hat, axis=-1, keepdims=True) - x_hat * jnp.mean(grad_hat * x_hat, axis=-1, keepdims=True))
    return d_row_vals, jnp.sum(grad_float * x_hat, axis=(0, 1)), jnp.sum(grad_float, axis=(0, 1))


def linear_rows(row_vals, weight, bias_vec):
    return jnp.einsum('btd,de->bte', row_vals, weight, preferred_element_type=jnp.float32) + bias_vec


def linear_back(d_out, weight):
    return jnp.einsum('bte,de->btd', d_out, weight, preferred_element_type=jnp.float32).astype(jnp.bfloat16)


def weight_grad(row_vals, d_out):
    return jnp.einsum('btd,bte->de', row_vals, d_out, preferred_element_type=jnp.float32)


def attention_forward(queries, key_rows, value_rows):
    scores = jnp.einsum('bqhd,bkhd->bhqk', queries, key_rows, preferred_element_type=jnp.float32) * ATTN_SCALE
    attn_prob = jax.nn.softmax(scores, axis=-1)
    prob_lo = attn_prob.astype(jnp.bfloat16)
    attn_out = jnp.einsum('bhqk,bkhd->bqhd', prob_lo, value_rows, preferred_element_type=jnp.float32)
    return attn_out.astype(jnp.bfloat16), attn_prob, prob_lo


def attention_backward(queries, key_rows, value_rows, attn_prob, prob_lo, d_attn):
    d_value = jnp.einsum('bhqk,bqhd->bkhd', prob_lo, d_attn, preferred_element_type=jnp.float32)
    d_prob = jnp.einsum('bqhd,bkhd->bhqk', d_attn, value_rows, preferred_element_type=jnp.float32).astype(jnp.bfloat16).astype(jnp.float32)
    d_scores = (attn_prob * (d_prob - jnp.sum(d_prob * attn_prob, axis=-1, keepdims=True)) * ATTN_SCALE).astype(jnp.bfloat16)
    d_query = jnp.einsum('bhqk,bkhd->bqhd', d_scores, key_rows, preferred_element_type=jnp.float32)
    d_key = jnp.einsum('bhqk,bqhd->bkhd', d_scores, queries, preferred_element_type=jnp.float32)
    return jnp.stack([d_query, d_key, d_value], axis=2).astype(jnp.bfloat16)


def solution(mesh):
    group_size = mesh.shape['sp']

    def local_block(x_special, x_patch, dy_special, dy_patch, ln_scale, ln_bias, w_qkv, b_qkv, w_proj, b_proj, layer_scale):
        num_images, special, d_model = x_special.shape
        patch_loc = x_patch.shape[1]
        num_heads = d_model // HEAD_DIM
        heads_loc = num_heads // group_size
        head_start = lax.axis_index('sp') * heads_loc

        normed_spec, value_a9, inv_spec = norm_forward(x_special, ln_scale, ln_bias)
        normed_patch, value_a10, inv_patch = norm_forward(x_patch, ln_scale, ln_bias)
        qkv_spec = linear_rows(normed_spec, w_qkv, b_qkv).astype(jnp.bfloat16).reshape(num_images, special, 3, num_heads, HEAD_DIM)
        qkv_patch = linear_rows(normed_patch, w_qkv, b_qkv).astype(jnp.bfloat16).reshape(num_images, patch_loc, 3, num_heads, HEAD_DIM)
        qkv_own = jnp.concatenate([
            lax.dynamic_slice_in_dim(qkv_spec, head_start, heads_loc, axis=3),
            lax.all_to_all(qkv_patch, 'sp', 3, 1, tiled=True)], axis=1)
        queries = qkv_own[:, :, 0]
        key_rows = qkv_own[:, :, 1]
        value_rows = qkv_own[:, :, 2]
        attn_own, attn_prob, prob_lo = attention_forward(queries, key_rows, value_rows)
        attn_spec = lax.all_gather(attn_own[:, :special], 'sp', axis=2, tiled=True).reshape(num_images, special, d_model)
        attn_patch = lax.all_to_all(attn_own[:, special:], 'sp', 1, 2, tiled=True).reshape(num_images, patch_loc, d_model)
        proj_spec = linear_rows(attn_spec, w_proj, b_proj)
        proj_patch = linear_rows(attn_patch, w_proj, b_proj)
        out_special = (x_special.astype(jnp.float32) + layer_scale * proj_spec).astype(jnp.bfloat16)
        out_patch = (x_patch.astype(jnp.float32) + layer_scale * proj_patch).astype(jnp.bfloat16)

        dy_spec = dy_special.astype(jnp.float32)
        dy_loc = dy_patch.astype(jnp.float32)
        d_proj_spec = dy_spec * layer_scale
        d_proj_patch = dy_loc * layer_scale
        d_proj_spec_lo = d_proj_spec.astype(jnp.bfloat16)
        d_proj_patch_lo = d_proj_patch.astype(jnp.bfloat16)
        d_attn_spec = linear_back(d_proj_spec_lo, w_proj).reshape(num_images, special, num_heads, HEAD_DIM)
        d_attn_patch = linear_back(d_proj_patch_lo, w_proj).reshape(num_images, patch_loc, num_heads, HEAD_DIM)
        d_attn_own = jnp.concatenate([
            lax.dynamic_slice_in_dim(d_attn_spec, head_start, heads_loc, axis=2),
            lax.all_to_all(d_attn_patch, 'sp', 2, 1, tiled=True)], axis=1)
        d_qkv_own = attention_backward(queries, key_rows, value_rows, attn_prob, prob_lo, d_attn_own)
        d_qkv_spec = lax.all_gather(d_qkv_own[:, :special], 'sp', axis=3, tiled=True).reshape(num_images, special, 3 * d_model)
        d_qkv_patch = lax.all_to_all(d_qkv_own[:, special:], 'sp', 1, 3, tiled=True).reshape(num_images, patch_loc, 3 * d_model)
        d_rows_spec, d_scale_spec, d_bias_spec = norm_backward(linear_back(d_qkv_spec, w_qkv), value_a9, inv_spec, ln_scale)
        d_rows_patch, d_scale_patch, d_bias_patch = norm_backward(linear_back(d_qkv_patch, w_qkv), value_a10, inv_patch, ln_scale)
        dx_special = (dy_spec + d_rows_spec).astype(jnp.bfloat16)
        dx_patch = (dy_loc + d_rows_patch).astype(jnp.bfloat16)

        patch_grads = lax.psum((
            d_scale_patch, d_bias_patch,
            weight_grad(normed_patch, d_qkv_patch),
            jnp.sum(d_qkv_patch, axis=(0, 1), dtype=jnp.float32),
            weight_grad(attn_patch, d_proj_patch_lo),
            jnp.sum(d_proj_patch, axis=(0, 1)),
            jnp.sum(dy_loc * proj_patch, axis=(0, 1))), 'sp')
        special_grads = (
            d_scale_spec, d_bias_spec,
            weight_grad(normed_spec, d_qkv_spec),
            jnp.sum(d_qkv_spec, axis=(0, 1), dtype=jnp.float32),
            weight_grad(attn_spec, d_proj_spec_lo),
            jnp.sum(d_proj_spec, axis=(0, 1)),
            jnp.sum(dy_spec * proj_spec, axis=(0, 1)))
        grad_list = tuple(summed + local_part for summed, local_part in zip(patch_grads, special_grads))
        return (out_special, out_patch, dx_special, dx_patch) + grad_list

    part_rows = P('dp')
    part_seq = P('dp', 'sp')
    replicated = P()
    return jax.shard_map(
        local_block, mesh=mesh,
        in_specs=(part_rows, part_seq, part_rows, part_seq, replicated, replicated, replicated, replicated, replicated, replicated, replicated),
        out_specs=(part_rows, part_seq, part_rows, part_seq, part_rows, part_rows, part_rows, part_rows, part_rows, part_rows, part_rows),
        check_vma=False)
```

profile of v0, /device:TPU:0, one launch (start us, length us, event | category | flops | bytes accessed | tf_op | source)
XLA Modules:
  0.0 1283.7 jit_solution(11548662308422552526)
XLA Ops:
  44.9 11.6 add_convert_fusion
  56.5 15.9 %reshape.169 = bf16[16,64,3,16,64]{4,3,2,1,0:T(8,128)(2,1)} reshape(bf16[16,64,3072]{2,1,0:T(8,128)(2,1)} %add_convert_fusion) | data formatting | bytes 12582912 | tf_op jit(solution)/shard_map/reshape | solution.py:68
  72.4 11.7 copy.102
  84.1 13.7 %reshape.183 = bf16[8,2,196608]{2,1,0:T(2,128)(2,1)} reshape(bf16[16,16,3,64,64]{4,3,2,1,0:T(8,128)(2,1)} %bitcast.118) | data formatting | bytes 12582912
  110.8 10.2 reshape.181
  142.7 99.2 %all-to-all-done = bf16[8,2,196608]{2,1,0:T(2,128)(2,1)} async-done(((bf16[8,2,196608]{2,1,0:T(2,128)(2,1)}), bf16[8,2,196608]{2,1,0:T(2,128)(2,1)}, u32[]{:S(2)}, u32[]{:S(2)}) %all-to-all-start) | async-done | bytes 6291488 | tf_op jit(solution)/shard_map/all_to_all | solution.py:71
  241.9 13.3 %reshape.184 = bf16[16,16,3,64,64]{4,3,2,1,0:T(8,128)(2,1)} reshape(bf16[8,2,196608]{2,1,0:T(2,128)(2,1)} %all-to-all-done) | data formatting | bytes 12582912
  255.3 17.2 %copy.78 = bf16[16,64,3,8,2,64]{1,3,5,4,0,2:T(8,128)(2,1)} copy(bf16[16,64,3,8,2,64]{5,1,2,0,4,3:T(8,128)(2,1)} %bitcast.119) | data formatting | bytes 12582912 | tf_op jit(solution)/shard_map/all_to_all | solution.py:71
  272.5 17.1 %all_to_all.51 = bf16[16,512,3,2,64]{1,4,3,0,2:T(8,128)(2,1)} reshape(bf16[16,8,64,3,2,64]{2,1,5,4,0,3:T(8,128)(2,1)} %bitcast.120) | data formatting | bytes 12582912 | tf_op jit(solution)/shard_map/all_to_all | solution.py:71
  295.7 19.8 %fusion.102 = (f32[16,2,513]{2,1,0:T(2,128)S(1)}, f32[16,2,513,513]{2,3,1,0:T(8,128)}) fusion(bf16[16,513,2,64]{1,3,2,0:T(8,128)(2,1)} %get-tuple-element.31, bf16[16,513,2,64]{1,3,2,0:T(8,128)(2,1)} %get-tuple-element.30), kind=kOutput, calls=%fused_computation.136 | convolution fusion | flops 1103204864 | bytes 37953792 | tf_op jit(solution)/shard_map/sub | solution.py:40
  315.5 17.8 %convert_bitcast_fusion.3 = bf16[16,513,2,64]{1,3,2,0:T(8,128)(2,1)} fusion(bf16[16,512,3,2,64]{1,4,3,0,2:T(8,128)(2,1)} %all_to_all.51, bf16[16,1,3,2,64]{1,4,3,0,2:T(8,128)(2,1)} %copy.97, f32[16,2,513,513]{2,3,1,0:T(8,128)} %get-tuple-element.37, f32[16,2,513]{2,1,0:T(2,128)S(1)} %get-tuple-element.36), kind=kOutput, calls=%fused_computation.77 | convolution fusion | flops 1100036096 | bytes 42156288 | tf_op jit(solution)/shard_map/bhqk,bkhd->bqhd/dot_general | solution.py:42
  337.5 10.7 copy.80
  360.4 17.9 %convert_bitcast_fusion = bf16[16,513,1,2,64]{1,4,3,0,2:T(8,128)(2,1)} fusion(bf16[16,512,2,64]{1,3,2,0:T(8,128)(2,1)} %all_to_all.58, bf16[16,1,2,64]{1,3,2,0:T(8,128)(2,1)S(1)} %constant_dynamic-slice_fusion, f32[16,2,513,513]{2,3,1,0:T(8,128)} %get-tuple-element.37, f32[16,2,513]{2,1,0:T(2,128)S(1)} %get-tuple-element.36), kind=kOutput, calls=%fused_computation.74 | convolution fusion | flops 1100036096 | bytes 37953792 | tf_op jit(solution)/shard_map/bhqk,bqhd->bkhd/dot_general | solution.py:47
  378.3 13.7 %convolution_convert_fusion = bf16[16,2,513,513]{2,3,1,0:T(8,128)(2,1)} fusion(bf16[16,512,2,64]{1,3,2,0:T(8,128)(2,1)} %all_to_all.58, bf16[16,1,2,64]{1,3,2,0:T(8,128)(2,1)S(1)} %constant_dynamic-slice_fusion, bf16[16,512,3,2,64]{1,4,3,0,2:T(8,128)(2,1)} %all_to_all.51, bf16[16,1,3,2,64]{1,4,3,0,2:T(8,128)(2,1)} %copy.97), kind=kOutput, calls=%fused_computation.19 | convolution fusion | flops 1094766592 | bytes 25247808 | tf_op jit(solution)/shard_map/bqhd,bkhd->bhqk/dot_general | solution.py:48
  392.0 44.0 %convert_bitcast_fusion.2 = bf16[16,513,1,2,64]{1,4,3,0,2:T(8,128)(2,1)} fusion(bf16[16,513,2,64]{1,3,2,0:T(8,128)(2,1)} %get-tuple-element.30, bf16[16,2,513,513]{2,3,1,0:T(8,128)(2,1)} %convolution_convert_fusion, f32[16,2,513,513]{2,3,1,0:T(8,128)} %get-tuple-element.37, f32[16,2,513]{2,1,0:T(2,128)S(1)} %get-tuple-element.36), kind=kOutput, calls=%fused_computation.76 | convolution fusion | flops 1154800384 | bytes 54796608 | tf_op jit(solution)/shard_map/bhqk,bkhd->bqhd/dot_general | solution.py:50
  436.0 54.3 %convert_bitcast_fusion.1 = bf16[16,513,1,2,64]{1,4,3,0,2:T(8,128)(2,1)} fusion(bf16[16,513,2,64]{1,3,2,0:T(8,128)(2,1)} %get-tuple-element.31, bf16[16,2,513,513]{2,3,1,0:T(8,128)(2,1)} %convolution_convert_fusion, f32[16,2,513,513]{2,3,1,0:T(8,128)} %get-tuple-element.37, f32[16,2,513]{2,1,0:T(2,128)S(1)} %get-tuple-element.36), kind=kOutput, calls=%fused_computation.75 | convolution fusion | flops 1154800384 | bytes 54796608 | tf_op jit(solution)/shard_map/bhqk,bqhd->bkhd/dot_general | solution.py:51
  500.5 29.8 %copy.89 = bf16[16,512,3,2,64]{4,3,0,2,1:T(2,128)(2,1)} copy(bf16[16,512,3,2,64]{1,4,3,0,2:T(8,128)(2,1)} %pad_maximum_fusion) | data formatting | bytes 12582912 | tf_op jit(solution)/shard_map/slice | solution.py:96
  530.3 13.7 %reshape.189 = bf16[8,2,196608]{2,1,0:T(2,128)(2,1)} reshape(bf16[512,3,16,2,64]{4,3,2,1,0:T(2,128)(2,1)} %bitcast.121) | data formatting | bytes 12582912
  564.8 10.2 reshape.171
  581.6 106.2 %all-to-all-done.3 = bf16[8,2,196608]{2,1,0:T(2,128)(2,1)} async-done(((bf16[8,2,196608]{2,1,0:T(2,128)(2,1)}), bf16[8,2,196608]{2,1,0:T(2,128)(2,1)}, u32[]{:S(2)}, u32[]{:S(2)}) %all-to-all-start.3) | async-done | bytes 6291488 | tf_op jit(solution)/shard_map/all_to_all | solution.py:96
  687.8 13.3 %reshape.190 = bf16[512,3,16,2,64]{4,3,2,1,0:T(2,128)(2,1)} reshape(bf16[8,2,196608]{2,1,0:T(2,128)(2,1)} %all-to-all-done.3) | data formatting | bytes 12582912
  701.1 32.7 %copy.90 = bf16[16,8,64,3,2,64]{2,1,5,4,0,3:T(8,128)(2,1)} copy(bf16[16,8,64,3,2,64]{5,4,0,3,2,1:T(2,128)(2,1)} %bitcast.122) | data formatting | bytes 12582912 | tf_op jit(solution)/shard_map/all_to_all | solution.py:96
  733.8 34.3 %copy.91 = bf16[16,64,3,8,2,64]{5,4,3,2,1,0:T(2,128)(2,1)} copy(bf16[16,64,3,8,2,64]{1,3,5,4,0,2:T(8,128)(2,1)} %bitcast.117) | data formatting | bytes 12582912 | tf_op jit(solution)/shard_map/all_to_all | solution.py:96
  768.1 16.4 %reshape.176 = bf16[16,64,3072]{2,1,0:T(8,128)(2,1)} reshape(bf16[16,64,3,8,2,64]{5,4,3,2,1,0:T(2,128)(2,1)} %copy.91) | data formatting | bytes 12582912 | tf_op jit(solution)/shard_map/reshape | solution.py:96
  784.5 12.9 %convolution_bitcast_fusion = f32[1024,3072]{1,0:T(8,128)} fusion(bf16[16,64,3072]{2,1,0:T(8,128)(2,1)} %reshape.176, bf16[16,64,1024]{2,1,0:T(8,128)(2,1)} %param.12, f32[1024]{0:T(1024)S(1)} %copy-done.16, f32[1024]{0:T(1024)S(1)} %copy-done.10, f32[16,64]{1,0:T(8,128)S(1)} %copy-done.21, f32[16,64]{1,0:T(8,128)S(1)} %copy-done.14), kind=kOutput, calls=%fused_computation.29 | convolution fusion | flops 6448742400 | bytes 20987904 | tf_op jit(solution)/shard_map/btd,bte->de/dot_general | solution.py:35
  798.5 69.4 %all_gather.6 = bf16[16,1,16,64]{1,3,2,0:T(8,128)(2,1)} all-gather(bf16[16,1,2,64]{1,3,2,0:T(8,128)(2,1)S(1)} %slice-done), channel_id=1, replica_groups=mesh['dp'=4,'sp'=8] {'sp'}, dimensions={2}, use_global_device_ids=true | all-gather | bytes 36864 | tf_op jit(solution)/shard_map/all_gather | solution.py:76
  874.0 181.6 %all_gather.7 = bf16[16,1,3,16,64]{1,4,3,0,2:T(8,128)(2,1)} all-gather(bf16[16,1,3,2,64]{1,4,3,0,2:T(8,128)(2,1)S(1)} %pad_maximum_fusion.6), channel_id=1, replica_groups=mesh['dp'=4,'sp'=8] {'sp'}, dimensions={3}, use_global_device_ids=true | all-gather | bytes 110592 | tf_op jit(solution)/shard_map/all_gather | solution.py:95
  1055.5 11.2 copy.88
  1087.2 12.1 fusion.42
  1105.2 32.3 %all-reduce = (f32[1024]{0:T(1024)S(1)}, f32[1024]{0:T(1024)S(1)}, f32[3072]{0:T(1024)S(1)}, f32[1024]{0:T(1024)S(1)}, f32[1024]{0:T(1024)S(1)}) all-reduce(f32[1024]{0:T(1024)S(1)} %get-tuple-element.11, f32[1024]{0:T(1024)S(1)} %get-tuple-element.16, f32[3072]{0:T(1024)S(1)} %reduce_sum.199, ...), channel_id=1, replica_groups=mesh['dp'=4,'sp'=8] {'sp'}, use_global_device_ids=true, to_apply=%region_12.0 | all-reduce | flops 7168 | bytes 57344 | tf_op jit(solution)/shard_map/psum | solution.py:102
  1140.5 121.8 %all-reduce.4.cloned.1.call-done = (f32[1024,3072]{1,0:T(8,128)}, f32[1024,1024]{1,0:T(8,128)}) async-done(((f32[1024,3072]{1,0:T(8,128)}, f32[1024,1024]{1,0:T(8,128)}), (f32[1024,3072]{1,0:T(8,128)}, f32[1024,1024]{1,0:T(8,128)})) %all-reduce.4.cloned.1.call-update) | async-done | bytes 16777232 | tf_op jit(solution)/shard_map/psum | solution.py:102
  1262.2 11.4 convolution_add_fusion
  (111 shorter events, 171.4 us)
Async XLA Ops:
  7.2 1.6 copy-start
  33.3 11.6 copy-start.9
  33.3 11.6 copy-start.15
  33.3 11.6 copy-start.19
  33.3 64.5 %all-to-all-start.2 = ((bf16[8,2,65536]{2,1,0:T(2,128)(2,1)}), bf16[8,2,65536]{2,1,0:T(2,128)(2,1)}, u32[]{:S(2)}, u32[]{:S(2)}) async-start(bf16[8,2,65536]{2,1,0:T(2,128)(2,1)} %reshape.187), calls=%async_computation.2 | async-start | bytes 4194304 | tf_op jit(solution)/shard_map/all_to_all | solution.py:93
  39.8 5.0 copy-start.1
  41.9 2.3 copy-start.13
  44.2 0.6 copy-start.20
  97.8 5.5 copy-start.5
  97.8 144.1 %all-to-all-start = ((bf16[8,2,196608]{2,1,0:T(2,128)(2,1)}), bf16[8,2,196608]{2,1,0:T(2,128)(2,1)}, u32[]{:S(2)}, u32[]{:S(2)}) async-start(bf16[8,2,196608]{2,1,0:T(2,128)(2,1)} %reshape.183), calls=%async_computation | async-start | bytes 12582912 | tf_op jit(solution)/shard_map/all_to_all | solution.py:71
  103.4 0.5 copy-start.17
  103.9 0.5 copy-start.22
  104.5 5.7 copy-start.7
  104.5 5.7 copy-start.11
  355.8 188.3 %all-to-all-start.1 = ((bf16[8,2,65536]{2,1,0:T(2,128)(2,1)}), bf16[8,2,65536]{2,1,0:T(2,128)(2,1)}, u32[]{:S(2)}, u32[]{:S(2)}) async-start(bf16[8,2,65536]{2,1,0:T(2,128)(2,1)} %reshape.185), calls=%async_computation.1 | async-start | bytes 4194304 | tf_op jit(solution)/shard_map/all_to_all | solution.py:77
  544.0 143.8 %all-to-all-start.3 = ((bf16[8,2,196608]{2,1,0:T(2,128)(2,1)}), bf16[8,2,196608]{2,1,0:T(2,128)(2,1)}, u32[]{:S(2)}, u32[]{:S(2)}) async-start(bf16[8,2,196608]{2,1,0:T(2,128)(2,1)} %reshape.189), calls=%async_computation.3 | async-start | bytes 12582912 | tf_op jit(solution)/shard_map/all_to_all | solution.py:96
  549.1 713.2 %all-reduce.4.cloned.1.call-start = ((), (), s32[]{:S(2)}) async-start(), calls=%async_computation.4 | async-start | bytes 33554432 | tf_op jit(solution)/shard_map/psum | solution.py:102
  564.8 10.2 copy-start.12
  768.1 16.4 %copy-start.10 = (f32[1024]{0:T(1024)S(1)}, f32[1024]{0:T(1024)}, u32[]{:S(2)}) copy-start(f32[1024]{0:T(1024)} %param.15) | copy-start | bytes 12292
  768.1 16.4 %copy-start.14 = (f32[16,64]{1,0:T(8,128)S(1)}, f32[16,64]{1,0:T(8,128)}, u32[]{:S(2)}) copy-start(f32[16,64]{1,0:T(8,128)} %copy-done.13) | copy-start | bytes 12292
  768.1 16.4 %copy-start.16 = (f32[1024]{0:T(1024)S(1)}, f32[1024]{0:T(1024)}, u32[]{:S(2)}) copy-start(f32[1024]{0:T(1024)} %param.16) | copy-start | bytes 12292
  768.1 16.4 %copy-start.21 = (f32[16,64]{1,0:T(8,128)S(1)}, f32[16,64]{1,0:T(8,128)}, u32[]{:S(2)}) copy-start(f32[16,64]{1,0:T(8,128)} %copy-done.20) | copy-start | bytes 12292
  797.4 1.0 slice-start
  1066.9 7.2 copy-start.6
  1066.9 7.2 copy-start.18
  1066.9 7.2 copy-start.23
  1074.0 4.9 copy-start.8
  1074.0 4.9 copy-start.24
  1087.2 12.1 copy-start.2
  1087.2 12.1 copy-start.4
  1087.2 12.1 copy-start.25
  1262.2 11.4 copy-start.3
Sparse Core Ops, SparseCore 0:
  797.6 464.6 all-reduce.3
where the time goes:
time: 1300 us; the launch traced here: 1280 us
  local copies, waits for them, and re-layouts  346 us (27%)
  waiting for transfers between devices  327 us (25%)
  blocking collectives  283 us (22%)
  matrix products  246 us (19%)
  other arithmetic  44.3 us (3%)
  starting transfers between devices  21.7 us (2%)
  between operations  14.8 us (1%)
    all_gather x1, blocking collectives, local_block(): lax.all_gather(d_qkv_own[:, :special], 'sp', axis=3, tiled=True)  182 us
    psum x1, waiting for transfers between devices, local_block(): lax.psum((d_scale_patch, d_bias_patch, weight_grad(normed_patch, d_qkv_pa...  122 us
    all_to_all x1, waiting for transfers between devices, local_block(): lax.all_to_all(d_qkv_own[:, special:], 'sp', 1, 3, tiled=True)  106 us
    all_to_all x1, waiting for transfers between devices, local_block(): lax.all_to_all(qkv_patch, 'sp', 3, 1, tiled=True)  99.2 us
    unnamed x61, local copies, waits for them, and re-layouts  89 us
    all_gather x1, blocking collectives, local_block(): lax.all_gather(attn_own[:, :special], 'sp', axis=2, tiled=True)  69.4 us
    all_to_all x2, local copies, waits for them, and re-layouts, local_block(): lax.all_to_all(d_qkv_own[:, special:], 'sp', 1, 3, tiled=True)  67 us
    dot_general x1, matrix products, attention_backward(): jnp.einsum('bhqk,bqhd->bkhd', d_scores, queries, preferred_element_type=j...  54.3 us
  transfers between devices with their start and end apart: 5, of which 3 were waited for; matrix products, arithmetic and copies ran while one was open for 28% of the time, Pallas kernels for 0%

commit v1 on v0

v1 whole, which is shorter than its diff:
```python
import functools

import jax
import jax.numpy as jnp
from jax import lax
from jax.experimental import pallas as pl
from jax.experimental.pallas import tpu as pltpu
from jax.sharding import PartitionSpec as P

HEAD_DIM = 64
LN_EPS = 1e-6
ATTN_SCALE = HEAD_DIM ** -0.5
LANES = 128
PAD = 16
CHUNK_TILES = 3
OFFSETS = (4, 3, 5, 2, 6, 1, 7)
MESH = pl.DeviceIdType.MESH
F32 = jnp.float32
BF16 = jnp.bfloat16
NEG = -1e30


def dot_nn(a, b):
    return lax.dot_general(a, b, (((1,), (0,)), ((), ())), preferred_element_type=F32)


def dot_nt(a, b):
    return lax.dot_general(a, b, (((1,), (1,)), ((), ())), preferred_element_type=F32)


def dot_tn(a, b):
    return lax.dot_general(a, b, (((0,), (0,)), ((), ())), preferred_element_type=F32)


def normalize(x):
    x = x.astype(F32)
    centered = x - jnp.mean(x, axis=-1, keepdims=True)
    inv = lax.rsqrt(jnp.mean(centered * centered, axis=-1, keepdims=True) + LN_EPS)
    return centered * inv, inv


def block_kernel(n_dev, special, x_hbm, dy_hbm, xs_ref, dys_ref, ln_s, ln_b, wq, wk, wv, bq, bk, bv, wp, b_proj, l_scale,
                 out_hbm, dx_hbm, grad_hbm, vec_hbm,
                 x_s, dy_s, h_s, dp_s, o_acc, dh_acc, q_s, k_s, v_s, da_s, a_s, dq_s, dk_s, dv_s, dwb, recv0, recv_a, recv_b, vbuf,
                 x_snd, x_rcv, dy_snd, dy_rcv, out_snd, out_rcv, dx_snd, dx_rcv, vec_snd, vec_rcv,
                 s0, r0, s_a, r_a, s_b, r_b, s_d, r_d, s_l, loc):
    step = pl.program_id(0)
    n_steps = pl.num_programs(0)
    me = lax.axis_index('sp')
    core = lax.rem(me, 2)
    chip = me // 2
    partner = me + 1 - 2 * core
    inner = (chip == 1) | (chip == 2)
    odd = lax.rem(chip, 2)
    near_a = me + 2 - 4 * odd
    near_b = lax.rem(me + 6 + 4 * odd, n_dev)
    imgs, rows, d_model = x_s.shape
    patches = rows - PAD
    loc_p = patches // n_dev
    half = dwb.shape[1] // 2
    chunk = rows // CHUNK_TILES

    def to(peer):
        return {'sp': peer}

    def remote(src, dst, snd, rcv, peer):
        return pltpu.make_async_remote_copy(src, dst, snd, rcv, device_id=to(peer), device_id_type=MESH)

    def scatter_in(src, dst, snd, rcv, d):
        peer = lax.rem(me + d, n_dev)
        return remote(src.at[pl.ds(peer * imgs, imgs)], dst.at[:, pl.ds(pl.multiple_of(me * loc_p, loc_p), loc_p)], snd.at[d], rcv.at[d], peer)

    def local_in(src, dst, sem):
        return pltpu.make_async_copy(src.at[pl.ds(me * imgs, imgs)], dst.at[:, pl.ds(pl.multiple_of(me * loc_p, loc_p), loc_p)], sem)

    def scatter_out(src, dst, snd, rcv, d):
        peer = lax.rem(me + d, n_dev)
        return remote(src.at[:, pl.ds(pl.multiple_of(peer * loc_p, loc_p), loc_p)], dst.at[pl.ds(me * imgs, imgs)], snd.at[d], rcv.at[d], peer)

    def local_out(src, dst, sem):
        return pltpu.make_async_copy(src.at[:, pl.ds(pl.multiple_of(me * loc_p, loc_p), loc_p)], dst.at[pl.ds(me * imgs, imgs)], sem)

    def vec_copy(d):
        peer = lax.rem(me + d, n_dev)
        return remote(vbuf, vec_hbm.at[me], vec_snd.at[d], vec_rcv.at[d], peer)

    def pair_copy(b):
        slot = lax.rem(b, 2)
        return remote(dwb.at[slot, pl.ds(pl.multiple_of((1 - core) * half, half), half)], recv0.at[b], s0.at[b], r0.at[b], partner)

    def up_copy(b):
        return remote(recv0.at[b], recv_a.at[b], s_a.at[b], r_a.at[b], near_a)

    def mid_copy(b):
        return remote(recv0.at[b], recv_b.at[b], s_b.at[b], r_b.at[b], near_b)

    def down_copy(b):
        return remote(recv_a.at[b], recv_a.at[b], s_a.at[b], r_a.at[b], near_a)

    def own_rows():
        return pl.ds(pl.multiple_of(core * half, half), half)

    def share_copy(b):
        return remote(recv_a.at[b], grad_hbm.at[b, own_rows()], s_d.at[b], r_d.at[b], partner)

    def keep_copy(b):
        return pltpu.make_async_copy(recv_a.at[b], grad_hbm.at[b, own_rows()], s_l.at[b])

    add_rows = half // 8

    def stage_pair(b):
        copy = pair_copy(b)
        copy.wait_recv()
        copy.wait_send()
        slot = lax.rem(b, 2)

        def body(t, carry):
            r = pl.multiple_of(t * add_rows, add_rows)
            recv0[b, pl.ds(r, add_rows)] += dwb[slot, pl.ds(pl.multiple_of(core * half + r, add_rows), add_rows)]
            return carry
        lax.fori_loop(0, 8, body, 0)

        @pl.when(jnp.logical_not(inner))
        def _():
            up_copy(b).start()

    def stage_up(b):
        up_copy(b).wait_recv()

        def body(t, carry):
            r = pl.multiple_of(t * add_rows, add_rows)
            recv0[b, pl.ds(r, add_rows)] += recv_a[b, pl.ds(r, add_rows)]
            return carry
        lax.fori_loop(0, 8, body, 0)
        mid_copy(b).start()

    def stage_mid(b):
        mid_copy(b).wait_recv()

        def body(t, carry):
            r = pl.multiple_of(t * add_rows, add_rows)
            recv_a[b, pl.ds(r, add_rows)] = recv0[b, pl.ds(r, add_rows)] + recv_b[b, pl.ds(r, add_rows)]
            return carry
        lax.fori_loop(0, 8, body, 0)
        down_copy(b).start()
        share_copy(b).start()
        keep_copy(b).start()

    def stage_down(b):
        down_copy(b).wait_recv()
        share_copy(b).start()
        keep_copy(b).start()

    def advance(g):
        @pl.when(jnp.logical_not(inner) & (g >= 3))
        def _():
            stage_down(g - 3)

        @pl.when(inner & (g >= 2) & (g < n_steps + 2))
        def _():
            stage_mid(g - 2)

        @pl.when(inner & (g >= 1) & (g < n_steps + 1))
        def _():
            stage_up(g - 1)

    @pl.when(step == 0)
    def _():
        barrier = pltpu.get_barrier_semaphore()
        for d in OFFSETS:
            pl.semaphore_signal(barrier, inc=1, device_id=to(lax.rem(me + d, n_dev)), device_id_type=MESH)
        pl.semaphore_wait(barrier, n_dev - 1)
        for d in OFFSETS:
            scatter_in(x_hbm, x_s, x_snd, x_rcv, d).start()
        for d in OFFSETS:
            scatter_in(dy_hbm, dy_s, dy_snd, dy_rcv, d).start()
        local_in(x_hbm, x_s, loc.at[0]).start()
        local_in(dy_hbm, dy_s, loc.at[1]).start()
        for i in range(imgs):
            x_s[i, patches:] = xs_ref[i]
            dy_s[i, patches:] = dys_ref[i]
        vbuf[...] = jnp.zeros_like(vbuf)
        local_in(x_hbm, x_s, loc.at[0]).wait()
        for d in OFFSETS:
            scatter_in(x_hbm, x_s, x_snd, x_rcv, d).wait_recv()

        def ln_body(t, carry):
            i, r = t // CHUNK_TILES, pl.multiple_of(lax.rem(t, CHUNK_TILES) * chunk, 16)
            x_hat, _ = normalize(x_s[i, pl.ds(r, chunk)])
            h_s[i, pl.ds(r, chunk)] = (x_hat * ln_s[...] + ln_b[...]).astype(BF16)
            o_acc[i, pl.ds(r, chunk)] = jnp.zeros((chunk, d_model), F32)
            dh_acc[i, pl.ds(r, chunk)] = jnp.zeros((chunk, d_model), F32)
            return carry
        lax.fori_loop(0, imgs * CHUNK_TILES, ln_body, 0)
        local_in(dy_hbm, dy_s, loc.at[1]).wait()
        for d in OFFSETS:
            scatter_in(dy_hbm, dy_s, dy_snd, dy_rcv, d).wait_recv()

        def dy_body(t, total):
            i, r = t // CHUNK_TILES, pl.multiple_of(lax.rem(t, CHUNK_TILES) * chunk, 16)
            d_proj = dy_s[i, pl.ds(r, chunk)].astype(F32) * l_scale[...]
            dp_s[i, pl.ds(r, chunk)] = d_proj.astype(BF16)
            return total + jnp.sum(d_proj, axis=0, keepdims=True)
        d_bias = lax.fori_loop(0, imgs * CHUNK_TILES, dy_body, jnp.zeros((1, d_model), F32))
        for c in range(8):
            vbuf[40 + c:41 + c] = d_bias[:, c * LANES:(c + 1) * LANES]
        for d in OFFSETS:
            scatter_in(x_hbm, x_s, x_snd, x_rcv, d).wait_send()
            scatter_in(dy_hbm, dy_s, dy_snd, dy_rcv, d).wait_send()

    def project(i, carry):
        h = h_s[i]
        q_s[i] = (dot_nn(h, wq[...]) + bq[...]).astype(BF16)
        k_s[i] = (dot_nn(h, wk[...]) + bk[...]).astype(BF16)
        v_s[i] = (dot_nn(h, wv[...]) + bv[...]).astype(BF16)
        da_s[i] = dot_nt(dp_s[i], wp[...]).astype(BF16)
        return carry
    lax.fori_loop(0, imgs, project, 0)

    lane = lax.broadcasted_iota(jnp.int32, (1, LANES), 1)
    zero = jnp.zeros((), BF16)

    def attend(i, carry):
        q, k, v, da = q_s[i], k_s[i], v_s[i], da_s[i]
        a = jnp.zeros((rows, LANES), F32)
        dq, dk, dv = a, a, a
        keep_col = lax.broadcasted_iota(jnp.int32, (1, rows), 1) < patches + special
        for t in range(LANES // HEAD_DIM):
            mine = (lane // HEAD_DIM) == t
            qm, km, vm, dam = (jnp.where(mine, y, zero) for y in (q, k, v, da))
            s = dot_nt(qm, k) * ATTN_SCALE
            s = jnp.where(keep_col, s, NEG)
            e = jnp.exp(s - jnp.max(s, axis=-1, keepdims=True))
            p = e * (1.0 / jnp.sum(e, axis=-1, keepdims=True))
            p_lo = p.astype(BF16)
            a = a + dot_nn(p_lo, vm)
            dv = dv + dot_tn(p_lo, dam)
            dp = dot_nt(dam, v).astype(BF16).astype(F32)
            ds = (p * (dp - jnp.sum(dp * p, axis=-1, keepdims=True)) * ATTN_SCALE).astype(BF16)
            dq = dq + dot_nn(ds, km)
            dk = dk + dot_tn(ds, qm)
        a_s[i] = a.astype(BF16)
        dq_s[i] = dq.astype(BF16)
        dk_s[i] = dk.astype(BF16)
        dv_s[i] = dv.astype(BF16)
        return carry
    lax.fori_loop(0, imgs, attend, 0)

    def back(i, carry):
        o_acc[i] += dot_nn(a_s[i], wp[...])
        dh_acc[i] += dot_nt(dq_s[i], wq[...]) + dot_nt(dk_s[i], wk[...]) + dot_nt(dv_s[i], wv[...])
        return carry
    lax.fori_loop(0, imgs, back, 0)

    slot = lax.rem(step, 2)
    for j, ref in enumerate((dq_s, dk_s, dv_s)):
        vbuf[pl.ds(j * 8 + step, 1)] = sum(jnp.sum(ref[i].astype(F32), axis=0, keepdims=True) for i in range(imgs))

    cols = 256

    def weight_grads(t, carry):
        c = pl.ds(pl.multiple_of(t * cols, cols), cols)
        for j, (left, right) in enumerate(((h_s, dq_s), (h_s, dk_s), (h_s, dv_s), (dp_s, a_s))):
            dwb[slot, c, j * LANES:(j + 1) * LANES] = sum(dot_tn(left[i, :, c], right[i]) for i in range(imgs))
        return carry
    lax.fori_loop(0, d_model // cols, weight_grads, 0)

    pair_copy(step).start()
    advance(step)
    stage_pair(step)

    @pl.when(step == n_steps - 1)
    def _():
        def out_body(t, total):
            i, r = t // CHUNK_TILES, pl.multiple_of(lax.rem(t, CHUNK_TILES) * chunk, 16)
            proj = o_acc[i, pl.ds(r, chunk)] + b_proj[...]
            h_s[i, pl.ds(r, chunk)] = (x_s[i, pl.ds(r, chunk)].astype(F32) + l_scale[...] * proj).astype(BF16)
            return total + jnp.sum(dy_s[i, pl.ds(r, chunk)].astype(F32) * proj, axis=0, keepdims=True)
        d_scale = lax.fori_loop(0, imgs * CHUNK_TILES, out_body, jnp.zeros((1, d_model), F32))
        for d in OFFSETS:
            scatter_out(h_s, out_hbm, out_snd, out_rcv, d).start()
        local_out(h_s, out_hbm, loc.at[2]).start()

        advance(n_steps)

        def dx_body(t, carry):
            t_scale, t_bias = carry
            i, r = t // CHUNK_TILES, pl.multiple_of(lax.rem(t, CHUNK_TILES) * chunk, 16)
            x_hat, inv = normalize(x_s[i, pl.ds(r, chunk)])
            grad = dh_acc[i, pl.ds(r, chunk)].astype(BF16).astype(F32)
            g_hat = grad * ln_s[...]
            d_row = inv * (g_hat - jnp.mean(g_hat, axis=-1, keepdims=True) - x_hat * jnp.mean(g_hat * x_hat, axis=-1, keepdims=True))
            dp_s[i, pl.ds(r, chunk)] = (dy_s[i, pl.ds(r, chunk)].astype(F32) + d_row).astype(BF16)
            return t_scale + jnp.sum(grad * x_hat, axis=0, keepdims=True), t_bias + jnp.sum(grad, axis=0, keepdims=True)
        none = jnp.zeros((1, d_model), F32)
        d_ln_s, d_ln_b = lax.fori_loop(0, imgs * CHUNK_TILES, dx_body, (none, none))
        for d in OFFSETS:
            scatter_out(dp_s, dx_hbm, dx_snd, dx_rcv, d).start()
        local_out(dp_s, dx_hbm, loc.at[3]).start()

        for c in range(8):
            part = slice(c * LANES, (c + 1) * LANES)
            vbuf[24 + c:25 + c] = d_ln_s[:, part]
            vbuf[32 + c:33 + c] = d_ln_b[:, part]
            vbuf[48 + c:49 + c] = d_scale[:, part]
            for i in range(imgs):
                vbuf[56 + 8 * i + c:57 + 8 * i + c] = h_s[i, patches:, part].astype(F32)[:1]
                vbuf[72 + 8 * i + c:73 + 8 * i + c] = dp_s[i, patches:, part].astype(F32)[:1]
        for d in OFFSETS:
            vec_copy(d).start()
        pltpu.make_async_copy(vbuf, vec_hbm.at[me], loc.at[4]).start()

        advance(n_steps + 1)
        advance(n_steps + 2)

        local_out(h_s, out_hbm, loc.at[2]).wait()
        local_out(dp_s, dx_hbm, loc.at[3]).wait()
        pltpu.make_async_copy(vbuf, vec_hbm.at[me], loc.at[4]).wait()
        for d in OFFSETS:
            scatter_out(h_s, out_hbm, out_snd, out_rcv, d).wait()
            scatter_out(dp_s, dx_hbm, dx_snd, dx_rcv, d).wait()
            vec_copy(d).wait()

        def drain(b, carry):
            up_copy(b).wait_send()

            @pl.when(inner)
            def _():
                mid_copy(b).wait_send()
            share_copy(b).wait()
            keep_copy(b).wait()
            return carry
        lax.fori_loop(0, n_steps, drain, 0)


def solution(mesh):
    n_dev = mesh.shape['sp']

    def local_block(x_special, x_patch, dy_special, dy_patch, ln_scale, ln_bias, w_qkv, b_qkv, w_proj, b_proj, layer_scale):
        num_images, special, d_model = x_special.shape
        loc_p = x_patch.shape[1]
        imgs = num_images // n_dev
        pairs = d_model // LANES
        rows = n_dev * loc_p + PAD
        me = lax.axis_index('sp')

        def own_special(arr):
            own = lax.dynamic_slice_in_dim(arr, me * imgs, imgs, axis=0)
            return jnp.pad(own, ((0, 0), (0, PAD - special), (0, 0)))

        def whole(shape):
            return pl.BlockSpec(shape, lambda g: (0,) * len(shape))

        any_spec = pl.BlockSpec(memory_space=pl.ANY)
        row = (1, d_model)
        w_specs = [pl.BlockSpec((d_model, LANES), functools.partial(lambda j, g: (0, j * pairs + g), j)) for j in range(3)]
        b_specs = [pl.BlockSpec((1, LANES), functools.partial(lambda j, g: (0, j * pairs + g), j)) for j in range(3)]
        dma = pltpu.SemaphoreType.DMA
        big = (imgs, rows, d_model)
        thin = (imgs, rows, LANES)
        half = d_model // 2
        slots = pltpu.VMEM((pairs, half, 4 * LANES), F32)
        out_p, dx_p, grads, vecs = pl.pallas_call(
            functools.partial(block_kernel, n_dev, special),
            grid=(pairs,),
            out_shape=(
                jax.ShapeDtypeStruct(x_patch.shape, BF16), jax.ShapeDtypeStruct(x_patch.shape, BF16),
                jax.ShapeDtypeStruct((pairs, d_model, 4 * LANES), F32), jax.ShapeDtypeStruct((n_dev, 88, LANES), F32)),
            in_specs=[any_spec, any_spec, whole((imgs, PAD, d_model)), whole((imgs, PAD, d_model)), whole(row), whole(row),
                      *w_specs, *b_specs, pl.BlockSpec((LANES, d_model), lambda g: (g, 0)), whole(row), whole(row)],
            out_specs=(any_spec,) * 4,
            scratch_shapes=[
                *[pltpu.VMEM(big, BF16)] * 4, *[pltpu.VMEM(big, F32)] * 2, *[pltpu.VMEM(thin, BF16)] * 8,
                pltpu.VMEM((2, d_model, 4 * LANES), F32), slots, slots, slots, pltpu.VMEM((88, LANES), F32),
                *[dma((n_dev,))] * 10, *[dma((pairs,))] * 9, dma((5,))],
            compiler_params=pltpu.CompilerParams(
                collective_id=0, has_side_effects=True, dimension_semantics=('arbitrary',), vmem_limit_bytes=67_000_000),
        )(x_patch, dy_patch, own_special(x_special), own_special(dy_special), ln_scale[None], ln_bias[None],
          w_qkv, w_qkv, w_qkv, b_qkv[None], b_qkv[None], b_qkv[None], w_proj, b_proj[None], layer_scale[None])

        d_w_qkv = jnp.transpose(grads[:, :, :3 * LANES].reshape(pairs, d_model, 3, LANES), (1, 2, 0, 3)).reshape(d_model, 3 * d_model)
        d_w_proj = jnp.transpose(grads[:, :, 3 * LANES:], (0, 2, 1)).reshape(d_model, d_model)
        sums = jnp.sum(vecs[:, :56], axis=0).reshape(7, d_model)
        lone = vecs[:, 56:].reshape(n_dev, 2, imgs, special, d_model).astype(BF16)
        out_s = lone[:, 0].reshape(x_special.shape)
        dx_s = lone[:, 1].reshape(x_special.shape)
        return (out_s, out_p, dx_s, dx_p, sums[3], sums[4], d_w_qkv, sums[:3].reshape(3 * d_model), d_w_proj, sums[5], sums[6])

    part_rows = P('dp')
    part_seq = P('dp', 'sp')
    replicated = P()
    return jax.shard_map(
        local_block, mesh=mesh,
        in_specs=(part_rows, part_seq, part_rows, part_seq, replicated, replicated, replicated, replicated, replicated, replicated, replicated),
        out_specs=(part_rows, part_seq, part_rows, part_seq, part_rows, part_rows, part_rows, part_rows, part_rows, part_rows, part_rows),
        check_vma=False)
```

time: 1300 us -> 495 us (0.38); the launches traced: 1280 us -> 495 us
  Pallas kernels: 0 us -> 427 us
  waiting for transfers between devices: 327 us -> 0 us
  blocking collectives: 283 us -> 0 us
  local copies, waits for them, and re-layouts: 346 us -> 66.3 us
  matrix products: 246 us -> 0 us
  other arithmetic: 44.3 us -> 0.96 us
  starting transfers between devices: 21.7 us -> 0 us
  between operations: 14.8 us -> 0.7 us
    pallas_call x0 -> x1, Pallas kernels: none -> 427 us  [local_block(): pl.pallas_call(functools.partial(block_kernel, n_dev, special), grid=(pai...]
    all_gather x2 -> x0, blocking collectives: 251 us -> none  [the longest x1 182 us: local_block(): lax.all_gather(d_qkv_own[:, :special], 'sp', axis=3, tiled=True)]
    dot_general x17 -> x0, matrix products: 226 us -> none  [the longest x1 54.3 us: attention_backward(): jnp.einsum('bhqk,bqhd->bkhd', d_scores, queries, preferred_element_type=j...]
    all_to_all x4 -> x0, waiting for transfers between devices: 205 us -> none  [the longest x1 106 us: local_block(): lax.all_to_all(d_qkv_own[:, special:], 'sp', 1, 3, tiled=True)]
    all_to_all x7 -> x0, local copies, waits for them, and re-layouts: 123 us -> none  [the longest x2 67 us: local_block(): lax.all_to_all(d_qkv_own[:, special:], 'sp', 1, 3, tiled=True)]
    psum x1 -> x0, waiting for transfers between devices: 122 us -> none  [local_block(): lax.psum((d_scale_patch, d_bias_patch, weight_grad(normed_patch, d_qkv_pa...]
    reshape x8 -> x1, local copies, waits for them, and re-layouts: 76.2 us -> 0.6 us  [local_block(): sums[:3].reshape(3 * d_model)]
    unnamed x61 -> x9, local copies, waits for them, and re-layouts: 89 us -> 16.3 us
  transfers between devices with their start and end apart: 5 -> 0, of which waited for: 3 -> 0; matrix products, arithmetic and copies ran while one was open for 28% -> 0% of each run, Pallas kernels for 0% -> 0%
where the time goes in v1:
time: 495 us
  Pallas kernels  427 us (86%)
  local copies, waits for them, and re-layouts  66.3 us (13%)
    pallas_call x1, Pallas kernels, local_block(): pl.pallas_call(functools.partial(block_kernel, n_dev, special), grid=(pai...  427 us
    slice x2, local copies, waits for them, and re-layouts, local_block(): grads[:, :, :3 * LANES].reshape(pairs, d_model, 3, LANES)  22.8 us
    unnamed x9, local copies, waits for them, and re-layouts  16.3 us
    transpose x1, local copies, waits for them, and re-layouts, local_block(): jnp.transpose(grads[:, :, :3 * LANES].reshape(pairs, d_model, 3, LANES),...  11.8 us
    transpose x2, local copies, waits for them, and re-layouts, local_block(): jnp.transpose(grads[:, :, 3 * LANES:], (0, 2, 1)).reshape(d_model, d_model)  9.92 us

profile of v1, /device:TPU:0, one launch (start us, length us, event | category | flops | bytes accessed | tf_op | source)
XLA Modules:
  0.0 494.6 jit_solution(8781209123177516353)
XLA Ops:
  0.6 0.8 constant_dynamic-slice_fusion
  1.4 0.6 pad.7.xs_ref
  2.1 0.6 pad.8.dys_ref
  2.7 426.7 %shard_map.194 = (bf16[16,64,1024]{2,1,0:T(8,128)(2,1)}, bf16[16,64,1024]{2,1,0:T(8,128)(2,1)}, f32[8,1024,512]{2,1,0:T(8,128)}, f32[8,88,128]{2,1,0:T(8,128)}) custom-call(bf16[16,64,1024]{2,1,0:T(8,128)(2,1)} %x_hbm.1, bf16[16,64,1024]{2,1,0:T(8,128)(2,1)} %dy_hbm.1, bf16[2,16,1024]{2,1,0:T(8,128)(2,1)} %pad.7.xs_ref, bf16[2,16,1024]{2,1,0:T(8,128)(2,1)} %pad.8.dys_ref, ...), custom_call_target="tpu_custom_call" | custom-call | tf_op jit(solution)/shard_map/pallas_call | solution.py:363
  429.4 1.0 slice_reduce_fusion
  430.4 0.9 slice.66
  431.4 0.6 reshape_squeeze.7
  432.0 0.6 slice_bitcast_fusion.1
  432.6 0.6 slice_bitcast_fusion.2
  433.2 0.6 reshape_squeeze.6
  433.8 4.4 slice_bitcast_fusion
  438.3 10.3 %slice.45 = f32[8,1024,384]{2,1,0:T(8,128)} slice(f32[8,1024,512]{2,1,0:T(8,128)} %get-tuple-element.18), slice={[0:8], [0:1024], [0:384]} | slice | bytes 25165824 | tf_op jit(solution)/shard_map/slice | solution.py:381
  448.5 12.6 %copy.31 = f32[8,1024,384]{1,2,0:T(8,128)} copy(f32[8,1024,384]{2,1,0:T(8,128)} %slice.45) | data formatting | bytes 25165824 | tf_op jit(solution)/shard_map/slice | solution.py:381
  461.1 11.8 %copy.32 = f32[1024,3,8,128]{0,3,2,1:T(8,128)} copy(f32[1024,3,8,128]{0,3,1,2:T(8,128)} %bitcast.26) | data formatting | bytes 25165824 | tf_op jit(solution)/shard_map/transpose | solution.py:381
  472.9 12.6 %copy.34 = f32[1024,3072]{1,0:T(8,128)} copy(f32[1024,3072]{0,1:T(8,128)} %bitcast.27) | data formatting | bytes 25165824
  485.5 0.0 copy-start.1
  485.5 5.5 %copy.33 = f32[8,128,1024]{2,1,0:T(8,128)} copy(f32[8,128,1024]{1,2,0:T(8,128)} %slice_bitcast_fusion) | data formatting | bytes 8388608 | tf_op jit(solution)/shard_map/transpose | solution.py:382
  491.0 0.0 copy-start
  491.0 0.0 copy-done.1
  491.0 1.3 copy.39
  492.3 1.0 copy-done
  493.3 1.3 copy.40
  (4 shorter events, 0.1 us)
Async XLA Ops:
  485.5 5.5 %copy-start.1 = (bf16[16,64,1024]{2,1,0:T(8,128)(2,1)S(1)}, bf16[16,64,1024]{2,1,0:T(8,128)(2,1)}, u32[]{:S(2)}) copy-start(bf16[16,64,1024]{2,1,0:T(8,128)(2,1)} %get-tuple-element.50) | copy-start | bytes 6291460
  491.0 2.3 copy-start

commit v2 on v1

v2 whole, which is shorter than its diff:
```python
import functools

import jax
import jax.numpy as jnp
from jax import lax
from jax.experimental import pallas as pl
from jax.experimental.pallas import tpu as pltpu
from jax.sharding import PartitionSpec as P

HEAD_DIM = 64
LN_EPS = 1e-6
ATTN_SCALE = HEAD_DIM ** -0.5
LANES = 128
PAD = 16
CHUNK_TILES = 3
SUBS = 2
MID_LAG = 2
DOWN_LAG = 4
OFFSETS = (4, 3, 5, 2, 6, 1, 7)
MESH = pl.DeviceIdType.MESH
F32 = jnp.float32
BF16 = jnp.bfloat16
NEG = -1e30


def dot_nn(a, b):
    return lax.dot_general(a, b, (((1,), (0,)), ((), ())), preferred_element_type=F32)


def dot_nt(a, b):
    return lax.dot_general(a, b, (((1,), (1,)), ((), ())), preferred_element_type=F32)


def dot_tn(a, b):
    return lax.dot_general(a, b, (((0,), (0,)), ((), ())), preferred_element_type=F32)


def normalize(x):
    x = x.astype(F32)
    centered = x - jnp.mean(x, axis=-1, keepdims=True)
    inv = lax.rsqrt(jnp.mean(centered * centered, axis=-1, keepdims=True) + LN_EPS)
    return centered * inv, inv


def block_kernel(n_dev, special, x_hbm, dy_hbm, xs_ref, dys_ref, ln_s, ln_b, wq, wk, wv, bq, bk, bv, wp, b_proj, l_scale,
                 out_hbm, dx_hbm, dwq_hbm, dwp_hbm, vec_hbm,
                 x_s, dy_s, h_s, dp_s, o_acc, dh_acc, w_s, qkv_s, g_s, da_s, a_s, dwb, recv0, recv_a, recv_b, vbuf,
                 x_snd, x_rcv, dy_snd, dy_rcv, out_snd, out_rcv, dx_snd, dx_rcv, vec_snd, vec_rcv,
                 s0, r0, s_a, r_a, s_b, r_b, s_d, r_d, s_l, loc):
    step = pl.program_id(0)
    n_steps = pl.num_programs(0)
    me = lax.axis_index('sp')
    core = lax.rem(me, 2)
    chip = me // 2
    partner = me + 1 - 2 * core
    inner = (chip == 1) | (chip == 2)
    odd = lax.rem(chip, 2)
    near_a = me + 2 - 4 * odd
    near_b = lax.rem(me + 6 + 4 * odd, n_dev)
    imgs, rows, d_model = x_s.shape
    patches = rows - PAD
    loc_p = patches // n_dev
    sub = dwb.shape[2]
    n_sub = SUBS * n_steps
    chunk = rows // CHUNK_TILES

    def to(peer):
        return {'sp': peer}

    def remote(src, dst, snd, rcv, peer):
        return pltpu.make_async_remote_copy(src, dst, snd, rcv, device_id=to(peer), device_id_type=MESH)

    def scatter_in(src, dst, snd, rcv, i, d):
        peer = lax.rem(me + d, n_dev)
        return remote(src.at[peer * imgs + i], dst.at[i, pl.ds(pl.multiple_of(me * loc_p, loc_p), loc_p)], snd.at[i, d], rcv.at[i, d], peer)

    def local_in(src, dst, snd, i):
        return pltpu.make_async_copy(src.at[me * imgs + i], dst.at[i, pl.ds(pl.multiple_of(me * loc_p, loc_p), loc_p)], snd.at[i, 0])

    def scatter_out(src, dst, snd, rcv, d):
        peer = lax.rem(me + d, n_dev)
        return remote(src.at[:, pl.ds(pl.multiple_of(peer * loc_p, loc_p), loc_p)], dst.at[pl.ds(me * imgs, imgs)], snd.at[d], rcv.at[d], peer)

    def local_out(src, dst, sem):
        return pltpu.make_async_copy(src.at[:, pl.ds(pl.multiple_of(me * loc_p, loc_p), loc_p)], dst.at[pl.ds(me * imgs, imgs)], sem)

    def vec_copy(d):
        peer = lax.rem(me + d, n_dev)
        return remote(vbuf, vec_hbm.at[me], vec_snd.at[d], vec_rcv.at[d], peer)

    def pair_copy(g):
        return remote(dwb.at[lax.rem(g, 2), pl.ds(SUBS * (1 - core), SUBS)], recv0.at[pl.ds(SUBS * g, SUBS)], s0.at[g], r0.at[g], partner)

    def up_copy(b):
        return remote(recv0.at[b], recv_a.at[b], s_a.at[b], r_a.at[b], near_a)

    def mid_copy(b):
        return remote(recv0.at[b], recv_b.at[b], s_b.at[b], r_b.at[b], near_b)

    def down_copy(b):
        return remote(recv_a.at[b], recv_a.at[b], s_a.at[b], r_a.at[b], near_a)

    def results(b):
        r = pl.ds(pl.multiple_of((SUBS * core + lax.rem(b, SUBS)) * sub, sub), sub)
        col = (b // SUBS) * LANES
        for j in range(4):
            src = recv_a.at[b, :, pl.ds(j * LANES, LANES)]
            c = pl.ds(pl.multiple_of(col + (j * d_model if j < 3 else 0), LANES), LANES)
            yield j, src, (dwq_hbm if j < 3 else dwp_hbm).at[r, c]

    def share_copies(b):
        return [remote(src, dst, s_d.at[b, j], r_d.at[b, j], partner) for j, src, dst in results(b)]

    def keep_copies(b):
        return [pltpu.make_async_copy(src, dst, s_l.at[b, j]) for j, src, dst in results(b)]

    def publish(b):
        for copy in share_copies(b) + keep_copies(b):
            copy.start()

    parts = 4
    add_rows = sub // parts

    def add_loop(add):
        def body(t, carry):
            add(pl.ds(pl.multiple_of(t * add_rows, add_rows), add_rows))
            return carry
        lax.fori_loop(0, parts, body, 0)

    def stage_pair(g):
        copy = pair_copy(g)
        copy.wait_recv()
        copy.wait_send()

        def one(t, carry):
            b = SUBS * g + t

            def add(r):
                recv0[b, r] += dwb[lax.rem(g, 2), SUBS * core + t, r]
            add_loop(add)

            @pl.when(jnp.logical_not(inner))
            def _():
                up_copy(b).start()
            return carry
        lax.fori_loop(0, SUBS, one, 0)

    def stage_up(b):
        up_copy(b).wait_recv()

        def add(r):
            recv0[b, r] += recv_a[b, r]
        add_loop(add)
        mid_copy(b).start()

    def stage_mid(b):
        mid_copy(b).wait_recv()

        def add(r):
            recv_a[b, r] = recv0[b, r] + recv_b[b, r]
        add_loop(add)
        down_copy(b).start()
        publish(b)

    def stage_down(b):
        down_copy(b).wait_recv()
        publish(b)

    def tick(t):
        @pl.when(inner & (t < n_sub))
        def _():
            stage_up(t)

        @pl.when(inner & (t >= MID_LAG) & (t < n_sub + MID_LAG))
        def _():
            stage_mid(t - MID_LAG)

        @pl.when(jnp.logical_not(inner) & (t >= DOWN_LAG))
        def _():
            stage_down(t - DOWN_LAG)

    arrivals = ((x_hbm, x_s, x_snd, x_rcv), (dy_hbm, dy_s, dy_snd, dy_rcv))

    @pl.when(step == 0)
    def _():
        barrier = pltpu.get_barrier_semaphore()
        for d in OFFSETS:
            pl.semaphore_signal(barrier, inc=1, device_id=to(lax.rem(me + d, n_dev)), device_id_type=MESH)
        pl.semaphore_wait(barrier, n_dev - 1)
        for i in range(imgs):
            for src, dst, snd, rcv in arrivals:
                for d in OFFSETS:
                    scatter_in(src, dst, snd, rcv, i, d).start()
                local_in(src, dst, snd, i).start()
        for i in range(imgs):
            x_s[i, patches:] = xs_ref[i]
            dy_s[i, patches:] = dys_ref[i]
        vbuf[...] = jnp.zeros_like(vbuf)

    def receive(src, dst, snd, rcv, i):
        local_in(src, dst, snd, i).wait()
        for d in OFFSETS:
            scatter_in(src, dst, snd, rcv, i, d).wait_recv()

    def prepare(i):
        receive(*arrivals[0], i)

        def ln_body(t, carry):
            r = pl.ds(pl.multiple_of(t * chunk, 16), chunk)
            x_hat, _ = normalize(x_s[i, r])
            h_s[i, r] = (x_hat * ln_s[...] + ln_b[...]).astype(BF16)
            o_acc[i, r] = jnp.zeros((chunk, d_model), F32)
            dh_acc[i, r] = jnp.zeros((chunk, d_model), F32)
            return carry
        lax.fori_loop(0, CHUNK_TILES, ln_body, 0)
        receive(*arrivals[1], i)

        def dy_body(t, total):
            r = pl.ds(pl.multiple_of(t * chunk, 16), chunk)
            d_proj = dy_s[i, r].astype(F32) * l_scale[...]
            dp_s[i, r] = d_proj.astype(BF16)
            return total + jnp.sum(d_proj, axis=0, keepdims=True)
        d_bias = lax.fori_loop(0, CHUNK_TILES, dy_body, jnp.zeros((1, d_model), F32))
        for c in range(8):
            vbuf[40 + c:41 + c] += d_bias[:, c * LANES:(c + 1) * LANES]

    bias = jnp.concatenate([bq[...], bk[...], bv[...]], axis=1)
    for j, ref in enumerate((wq, wk, wv)):
        w_s[:, j * LANES:(j + 1) * LANES] = ref[...]

    lane = lax.broadcasted_iota(jnp.int32, (1, LANES), 1)
    zero = jnp.zeros((), BF16)

    def attend(i, carry):
        @pl.when((i == imgs - 1) & (step >= 1))
        def _():
            tick(SUBS * step - 2)

        @pl.when(step == 0)
        def _():
            prepare(i)

        qkv_s[i] = (dot_nn(h_s[i], w_s[...]) + bias).astype(BF16)
        da_s[i] = dot_nt(dp_s[i], wp[...]).astype(BF16)
        q, k, v = (qkv_s[i, :, j * LANES:(j + 1) * LANES] for j in range(3))
        da = da_s[i]
        a = jnp.zeros((rows, LANES), F32)
        dq, dk, dv = a, a, a
        keep_col = lax.broadcasted_iota(jnp.int32, (1, rows), 1) < patches + special
        for t in range(LANES // HEAD_DIM):
            mine = (lane // HEAD_DIM) == t
            qm, km, vm, dam = (jnp.where(mine, y, zero) for y in (q, k, v, da))
            s = dot_nt(qm, k) * ATTN_SCALE
            s = jnp.where(keep_col, s, NEG)
            e = jnp.exp(s - jnp.max(s, axis=-1, keepdims=True))
            p = e * (1.0 / jnp.sum(e, axis=-1, keepdims=True))
            p_lo = p.astype(BF16)
            a = a + dot_nn(p_lo, vm)
            dv = dv + dot_tn(p_lo, dam)
            dp = dot_nt(dam, v).astype(BF16).astype(F32)
            ds = (p * (dp - jnp.sum(dp * p, axis=-1, keepdims=True)) * ATTN_SCALE).astype(BF16)
            dq = dq + dot_nn(ds, km)
            dk = dk + dot_tn(ds, qm)
        a_s[i] = a.astype(BF16)
        for j, grad in enumerate((dq, dk, dv)):
            g_s[i, :, j * LANES:(j + 1) * LANES] = grad.astype(BF16)
        return carry
    lax.fori_loop(0, imgs, attend, 0)

    slot = lax.rem(step, 2)
    d_qkv = sum(jnp.sum(g_s[i].astype(F32), axis=0, keepdims=True) for i in range(imgs))
    for j in range(3):
        vbuf[pl.ds(j * 8 + step, 1)] = d_qkv[:, j * LANES:(j + 1) * LANES]

    def weight_grads(t, carry):
        c = pl.ds(pl.multiple_of(t * sub, sub), sub)
        dwb[slot, t, :, :3 * LANES] = sum(dot_tn(h_s[i, :, c], g_s[i]) for i in range(imgs))
        dwb[slot, t, :, 3 * LANES:] = sum(dot_tn(dp_s[i, :, c], a_s[i]) for i in range(imgs))
        return carry
    lax.fori_loop(0, 2 * SUBS, weight_grads, 0)

    pair_copy(step).start()

    def back(i, carry):
        o_acc[i] += dot_nn(a_s[i], wp[...])
        dh_acc[i] += dot_nt(g_s[i], w_s[...])
        return carry
    lax.fori_loop(0, imgs, back, 0)

    @pl.when(step >= 1)
    def _():
        tick(SUBS * step - 1)
    stage_pair(step)

    @pl.when(step == n_steps - 1)
    def _():
        def out_body(t, total):
            i, r = t // CHUNK_TILES, pl.multiple_of(lax.rem(t, CHUNK_TILES) * chunk, 16)
            proj = o_acc[i, pl.ds(r, chunk)] + b_proj[...]
            h_s[i, pl.ds(r, chunk)] = (x_s[i, pl.ds(r, chunk)].astype(F32) + l_scale[...] * proj).astype(BF16)
            return total + jnp.sum(dy_s[i, pl.ds(r, chunk)].astype(F32) * proj, axis=0, keepdims=True)
        d_scale = lax.fori_loop(0, imgs * CHUNK_TILES, out_body, jnp.zeros((1, d_model), F32))
        for d in OFFSETS:
            scatter_out(h_s, out_hbm, out_snd, out_rcv, d).start()
        local_out(h_s, out_hbm, loc.at[2]).start()

        tick(n_sub - 2)

        def dx_body(t, carry):
            t_scale, t_bias = carry
            i, r = t // CHUNK_TILES, pl.multiple_of(lax.rem(t, CHUNK_TILES) * chunk, 16)
            x_hat, inv = normalize(x_s[i, pl.ds(r, chunk)])
            grad = dh_acc[i, pl.ds(r, chunk)].astype(BF16).astype(F32)
            g_hat = grad * ln_s[...]
            d_row = inv * (g_hat - jnp.mean(g_hat, axis=-1, keepdims=True) - x_hat * jnp.mean(g_hat * x_hat, axis=-1, keepdims=True))
            dp_s[i, pl.ds(r, chunk)] = (dy_s[i, pl.ds(r, chunk)].astype(F32) + d_row).astype(BF16)
            return t_scale + jnp.sum(grad * x_hat, axis=0, keepdims=True), t_bias + jnp.sum(grad, axis=0, keepdims=True)
        none = jnp.zeros((1, d_model), F32)
        d_ln_s, d_ln_b = lax.fori_loop(0, imgs * CHUNK_TILES, dx_body, (none, none))
        tick(n_sub - 1)
        for d in OFFSETS:
            scatter_out(dp_s, dx_hbm, dx_snd, dx_rcv, d).start()
        local_out(dp_s, dx_hbm, loc.at[3]).start()

        for c in range(8):
            part = slice(c * LANES, (c + 1) * LANES)
            vbuf[24 + c:25 + c] = d_ln_s[:, part]
            vbuf[32 + c:33 + c] = d_ln_b[:, part]
            vbuf[48 + c:49 + c] = d_scale[:, part]
            for i in range(imgs):
                vbuf[56 + 8 * i + c:57 + 8 * i + c] = h_s[i, patches:, part].astype(F32)[:1]
                vbuf[72 + 8 * i + c:73 + 8 * i + c] = dp_s[i, patches:, part].astype(F32)[:1]
        for d in OFFSETS:
            vec_copy(d).start()
        pltpu.make_async_copy(vbuf, vec_hbm.at[me], loc.at[4]).start()

        for t in range(DOWN_LAG):
            tick(n_sub + t)

        local_out(h_s, out_hbm, loc.at[2]).wait()
        local_out(dp_s, dx_hbm, loc.at[3]).wait()
        pltpu.make_async_copy(vbuf, vec_hbm.at[me], loc.at[4]).wait()
        for d in OFFSETS:
            for i in range(imgs):
                for src, dst, snd, rcv in arrivals:
                    scatter_in(src, dst, snd, rcv, i, d).wait_send()
            scatter_out(h_s, out_hbm, out_snd, out_rcv, d).wait()
            scatter_out(dp_s, dx_hbm, dx_snd, dx_rcv, d).wait()
            vec_copy(d).wait()

        def drain(b, carry):
            up_copy(b).wait_send()

            @pl.when(inner)
            def _():
                mid_copy(b).wait_send()
            for copy in share_copies(b) + keep_copies(b):
                copy.wait()
            return carry
        lax.fori_loop(0, n_sub, drain, 0)


def solution(mesh):
    n_dev = mesh.shape['sp']

    def local_block(x_special, x_patch, dy_special, dy_patch, ln_scale, ln_bias, w_qkv, b_qkv, w_proj, b_proj, layer_scale):
        num_images, special, d_model = x_special.shape
        loc_p = x_patch.shape[1]
        imgs = num_images // n_dev
        pairs = d_model // LANES
        rows = n_dev * loc_p + PAD
        me = lax.axis_index('sp')

        def own_special(arr):
            own = lax.dynamic_slice_in_dim(arr, me * imgs, imgs, axis=0)
            return jnp.pad(own, ((0, 0), (0, PAD - special), (0, 0)))

        def whole(shape):
            return pl.BlockSpec(shape, lambda g: (0,) * len(shape))

        any_spec = pl.BlockSpec(memory_space=pl.ANY)
        row = (1, d_model)
        w_specs = [pl.BlockSpec((d_model, LANES), functools.partial(lambda j, g: (0, j * pairs + g), j)) for j in range(3)]
        b_specs = [pl.BlockSpec((1, LANES), functools.partial(lambda j, g: (0, j * pairs + g), j)) for j in range(3)]
        dma = pltpu.SemaphoreType.DMA
        big = (imgs, rows, d_model)
        thin = (imgs, rows, LANES)
        sub = d_model // (2 * SUBS)
        slots = pltpu.VMEM((SUBS * pairs, sub, 4 * LANES), F32)
        wide = (imgs, rows, 3 * LANES)
        out_p, dx_p, d_w_qkv, d_w_proj_t, vecs = pl.pallas_call(
            functools.partial(block_kernel, n_dev, special),
            grid=(pairs,),
            out_shape=(
                jax.ShapeDtypeStruct(x_patch.shape, BF16), jax.ShapeDtypeStruct(x_patch.shape, BF16),
                jax.ShapeDtypeStruct((d_model, 3 * d_model), F32), jax.ShapeDtypeStruct((d_model, d_model), F32), jax.ShapeDtypeStruct((n_dev, 88, LANES), F32)),
            in_specs=[any_spec, any_spec, whole((imgs, PAD, d_model)), whole((imgs, PAD, d_model)), whole(row), whole(row),
                      *w_specs, *b_specs, pl.BlockSpec((LANES, d_model), lambda g: (g, 0)), whole(row), whole(row)],
            out_specs=(any_spec,) * 5,
            scratch_shapes=[
                *[pltpu.VMEM(big, BF16)] * 4, *[pltpu.VMEM(big, F32)] * 2, pltpu.VMEM((d_model, 3 * LANES), BF16), *[pltpu.VMEM(wide, BF16)] * 2, *[pltpu.VMEM(thin, BF16)] * 2,
                pltpu.VMEM((2, 2 * SUBS, sub, 4 * LANES), F32), slots, slots, slots, pltpu.VMEM((88, LANES), F32),
                *[dma((imgs, n_dev))] * 4, *[dma((n_dev,))] * 6, *[dma((pairs,))] * 2, *[dma((SUBS * pairs,))] * 4, *[dma((SUBS * pairs, 4))] * 3, dma((5,))],
            compiler_params=pltpu.CompilerParams(
                collective_id=0, has_side_effects=True, dimension_semantics=('arbitrary',), vmem_limit_bytes=67_000_000),
        )(x_patch, dy_patch, own_special(x_special), own_special(dy_special), ln_scale[None], ln_bias[None],
          w_qkv, w_qkv, w_qkv, b_qkv[None], b_qkv[None], b_qkv[None], w_proj, b_proj[None], layer_scale[None])

        d_w_proj = d_w_proj_t.T
        sums = jnp.sum(vecs[:, :56], axis=0).reshape(7, d_model)
        lone = vecs[:, 56:].reshape(n_dev, 2, imgs, special, d_model).astype(BF16)
        out_s = lone[:, 0].reshape(x_special.shape)
        dx_s = lone[:, 1].reshape(x_special.shape)
        return (out_s, out_p, dx_s, dx_p, sums[3], sums[4], d_w_qkv, sums[:3].reshape(3 * d_model), d_w_proj, sums[5], sums[6])

    part_rows = P('dp')
    part_seq = P('dp', 'sp')
    replicated = P()
    return jax.shard_map(
        local_block, mesh=mesh,
        in_specs=(part_rows, part_seq, part_rows, part_seq, replicated, replicated, replicated, replicated, replicated, replicated, replicated),
        out_specs=(part_rows, part_seq, part_rows, part_seq, part_rows, part_rows, part_rows, part_rows, part_rows, part_rows, part_rows),
        check_vma=False)
```

time: 495 us -> 429 us (0.87)
  local copies, waits for them, and re-layouts: 66.3 us -> 25.6 us
  Pallas kernels: 427 us -> 401 us
    pallas_call x1, Pallas kernels: 427 us -> 401 us  [local_block(): pl.pallas_call(functools.partial(block_kernel, n_dev, special), grid=(pai...]
    slice x2 -> x0, local copies, waits for them, and re-layouts: 22.8 us -> none  [local_block(): grads[:, :, :3 * LANES].reshape(pairs, d_model, 3, LANES)]
    transpose x3 -> x0, local copies, waits for them, and re-layouts: 21.7 us -> none  [the longest x1 11.8 us: local_block(): jnp.transpose(grads[:, :, :3 * LANES].reshape(pairs, d_model, 3, LANES),...]
    unnamed x9 -> x10, local copies, waits for them, and re-layouts: 16.3 us -> 20.2 us
where the time goes in v2:
time: 429 us
  Pallas kernels  401 us (93%)
  local copies, waits for them, and re-layouts  25.6 us (6%)
    pallas_call x1, Pallas kernels, local_block(): pl.pallas_call(functools.partial(block_kernel, n_dev, special), grid=(pai...  401 us
    unnamed x10, local copies, waits for them, and re-layouts  20.2 us

profile of v2, /device:TPU:0, one launch (start us, length us, event | category | flops | bytes accessed | tf_op | source)
XLA Modules:
  0.0 428.8 jit_solution(17613335909316983601)
XLA Ops:
  0.6 0.8 constant_dynamic-slice_fusion
  1.4 0.6 pad.7.xs_ref
  2.1 0.6 pad.8.dys_ref
  2.7 401.4 %shard_map.194 = (bf16[16,64,1024]{2,1,0:T(8,128)(2,1)}, bf16[16,64,1024]{2,1,0:T(8,128)(2,1)}, f32[1024,3072]{1,0:T(8,128)}, f32[1024,1024]{1,0:T(8,128)}, f32[8,88,128]{2,1,0:T(8,128)}) custom-call(bf16[16,64,1024]{2,1,0:T(8,128)(2,1)} %x_hbm.1, bf16[16,64,1024]{2,1,0:T(8,128)(2,1)} %dy_hbm.1, bf16[2,16,1024]{2,1,0:T(8,128)(2,1)} %pad.7.xs_ref, ...), custom_call_target="tpu_custom_call" | custom-call | tf_op jit(solution)/shard_map/pallas_call | solution.py:391
  404.2 1.0 slice_reduce_fusion
  405.1 0.9 slice.57
  406.1 0.6 reshape_squeeze.7
  406.8 0.6 slice_bitcast_fusion
  407.4 0.6 slice_bitcast_fusion.1
  408.0 0.6 reshape_squeeze.6
  408.6 0.0 copy-start.1
  408.6 5.5 %copy.24 = f32[1024,1024]{1,0:T(8,128)} copy(f32[1024,1024]{0,1:T(8,128)} %bitcast.20) | data formatting | bytes 8388608
  414.1 0.0 copy-done.1
  414.1 0.0 copy-start
  414.1 1.3 copy.30
  415.4 1.0 copy-done
  416.4 1.3 copy.31
  417.8 11.0 %copy.32 = f32[1024,3072]{1,0:T(8,128)} copy(f32[1024,3072]{1,0:T(8,128)} %get-tuple-element.57) | data formatting | bytes 25165824
  (4 shorter events, 0.1 us)
Async XLA Ops:
  408.6 5.5 %copy-start.1 = (bf16[16,64,1024]{2,1,0:T(8,128)(2,1)S(1)}, bf16[16,64,1024]{2,1,0:T(8,128)(2,1)}, u32[]{:S(2)}) copy-start(bf16[16,64,1024]{2,1,0:T(8,128)(2,1)} %get-tuple-element.52) | copy-start | bytes 6291460
  414.1 2.3 copy-start

commit v3 on v2

--- a/solution.py
+++ b/solution.py
@@ -14,8 +14,9 @@
 PAD = 16
 CHUNK_TILES = 3
 SUBS = 2
+PIECES = 2
 MID_LAG = 2
-DOWN_LAG = 4
+DOWN_LAG = 8
 OFFSETS = (4, 3, 5, 2, 6, 1, 7)
 MESH = pl.DeviceIdType.MESH
 F32 = jnp.float32
@@ -44,7 +45,7 @@
 
 def block_kernel(n_dev, special, x_hbm, dy_hbm, xs_ref, dys_ref, ln_s, ln_b, wq, wk, wv, bq, bk, bv, wp, b_proj, l_scale,
                  out_hbm, dx_hbm, dwq_hbm, dwp_hbm, vec_hbm,
-                 x_s, dy_s, h_s, dp_s, o_acc, dh_acc, w_s, qkv_s, g_s, da_s, a_s, dwb, recv0, recv_a, recv_b, vbuf,
+                 x_s, dy_s, h_s, dp_s, o_acc, dh_acc, w_s, qkv_s, g_s, da_s, a_s, p_s, dwb, recv0, recv_a, recv_b, vbuf,
                  x_snd, x_rcv, dy_snd, dy_rcv, out_snd, out_rcv, dx_snd, dx_rcv, vec_snd, vec_rcv,
                  s0, r0, s_a, r_a, s_b, r_b, s_d, r_d, s_l, loc):
     step = pl.program_id(0)
@@ -91,14 +92,17 @@
     def pair_copy(g):
         return remote(dwb.at[lax.rem(g, 2), pl.ds(SUBS * (1 - core), SUBS)], recv0.at[pl.ds(SUBS * g, SUBS)], s0.at[g], r0.at[g], partner)
 
-    def up_copy(b):
-        return remote(recv0.at[b], recv_a.at[b], s_a.at[b], r_a.at[b], near_a)
-
-    def mid_copy(b):
-        return remote(recv0.at[b], recv_b.at[b], s_b.at[b], r_b.at[b], near_b)
+    def piece(h):
+        return pl.ds(h * (sub // PIECES), sub // PIECES)
+
+    def up_copy(b, h):
+        return remote(recv0.at[b, piece(h)], recv_a.at[b, piece(h)], s_a.at[b, h], r_a.at[b, h], near_a)
+
+    def mid_copy(b, h):
+        return remote(recv0.at[b, piece(h)], recv_b.at[b, piece(h)], s_b.at[b, h], r_b.at[b, h], near_b)
 
     def down_copy(b):
-        return remote(recv_a.at[b], recv_a.at[b], s_a.at[b], r_a.at[b], near_a)
+        return remote(recv_a.at[b], recv_a.at[b], s_a.at[b, 0], r_a.at[b, 0], near_a)
 
     def results(b):
         r = pl.ds(pl.multiple_of((SUBS * core + lax.rem(b, SUBS)) * sub, sub), sub)
@@ -118,12 +122,12 @@
         for copy in share_copies(b) + keep_copies(b):
             copy.start()
 
-    parts = 4
-    add_rows = sub // parts
-
-    def add_loop(add):
+    parts = 2
+    add_rows = sub // (PIECES * parts)
+
+    def add_loop(h, add):
         def body(t, carry):
-            add(pl.ds(pl.multiple_of(t * add_rows, add_rows), add_rows))
+            add(pl.ds(pl.multiple_of(h * (sub // PIECES) + t * add_rows, add_rows), add_rows))
             return carry
         lax.fori_loop(0, parts, body, 0)
 
@@ -137,28 +141,29 @@
 
             def add(r):
                 recv0[b, r] += dwb[lax.rem(g, 2), SUBS * core + t, r]
-            add_loop(add)
-
-            @pl.when(jnp.logical_not(inner))
-            def _():
-                up_copy(b).start()
+            for h in range(PIECES):
+                add_loop(h, add)
+
+                @pl.when(jnp.logical_not(inner))
+                def _():
+                    up_copy(b, h).start()
             return carry
         lax.fori_loop(0, SUBS, one, 0)
 
     def stage_up(b):
-        up_copy(b).wait_recv()
-
         def add(r):
             recv0[b, r] += recv_a[b, r]
-        add_loop(add)
-        mid_copy(b).start()
+        for h in range(PIECES):
+            up_copy(b, h).wait_recv()
+            add_loop(h, add)
+            mid_copy(b, h).start()
 
     def stage_mid(b):
-        mid_copy(b).wait_recv()
-
         def add(r):
             recv_a[b, r] = recv0[b, r] + recv_b[b, r]
-        add_loop(add)
+        for h in range(PIECES):
+            mid_copy(b, h).wait_recv()
+            add_loop(h, add)
         down_copy(b).start()
         publish(b)
 
@@ -202,7 +207,7 @@
         for d in OFFSETS:
             scatter_in(src, dst, snd, rcv, i, d).wait_recv()
 
-    def prepare(i):
+    def prepare_rows(i):
         receive(*arrivals[0], i)
 
         def ln_body(t, carry):
@@ -213,6 +218,8 @@
             dh_acc[i, r] = jnp.zeros((chunk, d_model), F32)
             return carry
         lax.fori_loop(0, CHUNK_TILES, ln_body, 0)
+
+    def prepare_back(i):
         receive(*arrivals[1], i)
 
         def dy_body(t, total):
@@ -238,25 +245,32 @@
 
         @pl.when(step == 0)
         def _():
-            prepare(i)
+            prepare_rows(i)
 
         qkv_s[i] = (dot_nn(h_s[i], w_s[...]) + bias).astype(BF16)
-        da_s[i] = dot_nt(dp_s[i], wp[...]).astype(BF16)
         q, k, v = (qkv_s[i, :, j * LANES:(j + 1) * LANES] for j in range(3))
-        da = da_s[i]
         a = jnp.zeros((rows, LANES), F32)
         dq, dk, dv = a, a, a
         keep_col = lax.broadcasted_iota(jnp.int32, (1, rows), 1) < patches + special
-        for t in range(LANES // HEAD_DIM):
-            mine = (lane // HEAD_DIM) == t
-            qm, km, vm, dam = (jnp.where(mine, y, zero) for y in (q, k, v, da))
-            s = dot_nt(qm, k) * ATTN_SCALE
+        heads = [(lane // HEAD_DIM) == t for t in range(LANES // HEAD_DIM)]
+        for t, mine in enumerate(heads):
+            s = dot_nt(jnp.where(mine, q, zero), k) * ATTN_SCALE
             s = jnp.where(keep_col, s, NEG)
             e = jnp.exp(s - jnp.max(s, axis=-1, keepdims=True))
             p = e * (1.0 / jnp.sum(e, axis=-1, keepdims=True))
-            p_lo = p.astype(BF16)
-            a = a + dot_nn(p_lo, vm)
-            dv = dv + dot_tn(p_lo, dam)
+            p_s[t] = p
+            a = a + dot_nn(p.astype(BF16), jnp.where(mine, v, zero))
+
+        @pl.when(step == 0)
+        def _():
+            prepare_back(i)
+
+        da_s[i] = dot_nt(dp_s[i], wp[...]).astype(BF16)
+        da = da_s[i]
+        for t, mine in enumerate(heads):
+            qm, km, dam = (jnp.where(mine, y, zero) for y in (q, k, da))
+            p = p_s[t]
+            dv = dv + dot_tn(p.astype(BF16), dam)
             dp = dot_nt(dam, v).astype(BF16).astype(F32)
             ds = (p * (dp - jnp.sum(dp * p, axis=-1, keepdims=True)) * ATTN_SCALE).astype(BF16)
             dq = dq + dot_nn(ds, km)
@@ -268,18 +282,20 @@
     lax.fori_loop(0, imgs, attend, 0)
 
     slot = lax.rem(step, 2)
-    d_qkv = sum(jnp.sum(g_s[i].astype(F32), axis=0, keepdims=True) for i in range(imgs))
-    for j in range(3):
-        vbuf[pl.ds(j * 8 + step, 1)] = d_qkv[:, j * LANES:(j + 1) * LANES]
-
-    def weight_grads(t, carry):
+    def weight_grads(n, carry):
+        t = lax.rem(n + SUBS * (1 - core), 2 * SUBS)
         c = pl.ds(pl.multiple_of(t * sub, sub), sub)
         dwb[slot, t, :, :3 * LANES] = sum(dot_tn(h_s[i, :, c], g_s[i]) for i in range(imgs))
         dwb[slot, t, :, 3 * LANES:] = sum(dot_tn(dp_s[i, :, c], a_s[i]) for i in range(imgs))
         return carry
-    lax.fori_loop(0, 2 * SUBS, weight_grads, 0)
-
+    lax.fori_loop(0, SUBS, weight_grads, 0)
     pair_copy(step).start()
+    lax.fori_loop(SUBS, 2 * SUBS, weight_grads, 0)
+
+    d_qkv = sum(jnp.sum(g_s[i].astype(F32), axis=0, keepdims=True) for i in range(imgs))
+    for j in range(3):
+        vbuf[pl.ds(j * 8 + step, 1)] = d_qkv[:, j * LANES:(j + 1) * LANES]
+
 
     def back(i, carry):
         o_acc[i] += dot_nn(a_s[i], wp[...])
@@ -349,11 +365,16 @@
             vec_copy(d).wait()
 
         def drain(b, carry):
-            up_copy(b).wait_send()
-
             @pl.when(inner)
             def _():
-                mid_copy(b).wait_send()
+                down_copy(b).wait_send()
+                for h in range(PIECES):
+                    mid_copy(b, h).wait_send()
+
+            @pl.when(jnp.logical_not(inner))
+            def _():
+                for h in range(PIECES):
+                    up_copy(b, h).wait_send()
             for copy in share_copies(b) + keep_copies(b):
                 copy.wait()
             return carry
@@ -398,9 +419,9 @@
                       *w_specs, *b_specs, pl.BlockSpec((LANES, d_model), lambda g: (g, 0)), whole(row), whole(row)],
             out_specs=(any_spec,) * 5,
             scratch_shapes=[
-                *[pltpu.VMEM(big, BF16)] * 4, *[pltpu.VMEM(big, F32)] * 2, pltpu.VMEM((d_model, 3 * LANES), BF16), *[pltpu.VMEM(wide, BF16)] * 2, *[pltpu.VMEM(thin, BF16)] * 2,
+                *[pltpu.VMEM(big, BF16)] * 4, *[pltpu.VMEM(big, F32)] * 2, pltpu.VMEM((d_model, 3 * LANES), BF16), *[pltpu.VMEM(wide, BF16)] * 2, *[pltpu.VMEM(thin, BF16)] * 2, pltpu.VMEM((LANES // HEAD_DIM, rows, rows), F32),
                 pltpu.VMEM((2, 2 * SUBS, sub, 4 * LANES), F32), slots, slots, slots, pltpu.VMEM((88, LANES), F32),
-                *[dma((imgs, n_dev))] * 4, *[dma((n_dev,))] * 6, *[dma((pairs,))] * 2, *[dma((SUBS * pairs,))] * 4, *[dma((SUBS * pairs, 4))] * 3, dma((5,))],
+                *[dma((imgs, n_dev))] * 4, *[dma((n_dev,))] * 6, *[dma((pairs,))] * 2, *[dma((SUBS * pairs, PIECES))] * 4, *[dma((SUBS * pairs, 4))] * 3, dma((5,))],
             compiler_params=pltpu.CompilerParams(
                 collective_id=0, has_side_effects=True, dimension_semantics=('arbitrary',), vmem_limit_bytes=67_000_000),
         )(x_patch, dy_patch, own_special(x_special), own_special(dy_special), ln_scale[None], ln_bias[None],

time: 429 us -> 427 us (level)
  no operation moved by 1% of the time
where the time goes in v3:
time: 427 us
  Pallas kernels  399 us (93%)
  local copies, waits for them, and re-layouts  25.7 us (6%)
    pallas_call x1, Pallas kernels, local_block(): pl.pallas_call(functools.partial(block_kernel, n_dev, special), grid=(pai...  399 us
    unnamed x10, local copies, waits for them, and re-layouts  20.2 us

profile of v3, /device:TPU:0, one launch (start us, length us, event | category | flops | bytes accessed | tf_op | source)
XLA Modules:
  0.0 426.6 jit_solution(4274863606724587298)
XLA Ops:
  0.6 0.8 constant_dynamic-slice_fusion
  1.4 0.6 pad.7.xs_ref
  2.1 0.6 pad.8.dys_ref
  2.7 399.3 %shard_map.194 = (bf16[16,64,1024]{2,1,0:T(8,128)(2,1)}, bf16[16,64,1024]{2,1,0:T(8,128)(2,1)}, f32[1024,3072]{1,0:T(8,128)}, f32[1024,1024]{1,0:T(8,128)}, f32[8,88,128]{2,1,0:T(8,128)}) custom-call(bf16[16,64,1024]{2,1,0:T(8,128)(2,1)} %x_hbm.1, bf16[16,64,1024]{2,1,0:T(8,128)(2,1)} %dy_hbm.1, bf16[2,16,1024]{2,1,0:T(8,128)(2,1)} %pad.7.xs_ref, ...), custom_call_target="tpu_custom_call" | custom-call | tf_op jit(solution)/shard_map/pallas_call | solution.py:412
  402.0 1.0 slice_reduce_fusion
  403.0 0.9 slice.57
  404.0 0.6 reshape_squeeze.7
  404.6 0.6 slice_bitcast_fusion
  405.2 0.6 slice_bitcast_fusion.1
  405.8 0.6 reshape_squeeze.6
  406.5 0.0 copy-start.1
  406.5 5.5 %copy.24 = f32[1024,1024]{1,0:T(8,128)} copy(f32[1024,1024]{0,1:T(8,128)} %bitcast.20) | data formatting | bytes 8388608
  411.9 0.0 copy-done.1
  411.9 0.0 copy-start
  411.9 1.3 copy.30
  413.3 1.0 copy-done
  414.3 1.3 copy.31
  415.6 11.0 %copy.32 = f32[1024,3072]{1,0:T(8,128)} copy(f32[1024,3072]{1,0:T(8,128)} %get-tuple-element.57) | data formatting | bytes 25165824
  (4 shorter events, 0.1 us)
Async XLA Ops:
  406.5 5.5 %copy-start.1 = (bf16[16,64,1024]{2,1,0:T(8,128)(2,1)S(1)}, bf16[16,64,1024]{2,1,0:T(8,128)(2,1)}, u32[]{:S(2)}) copy-start(bf16[16,64,1024]{2,1,0:T(8,128)(2,1)} %get-tuple-element.52) | copy-start | bytes 6291460
  411.9 2.3 copy-start

commit v4 on v3

--- a/solution.py
+++ b/solution.py
@@ -15,7 +15,7 @@
 CHUNK_TILES = 3
 SUBS = 2
 PIECES = 2
-MID_LAG = 2
+MID_LAG = 3
 DOWN_LAG = 8
 OFFSETS = (4, 3, 5, 2, 6, 1, 7)
 MESH = pl.DeviceIdType.MESH
@@ -303,10 +303,11 @@
         return carry
     lax.fori_loop(0, imgs, back, 0)
 
+    stage_pair(step)
+
     @pl.when(step >= 1)
     def _():
         tick(SUBS * step - 1)
-    stage_pair(step)
 
     @pl.when(step == n_steps - 1)
     def _():
@@ -333,10 +334,6 @@
             return t_scale + jnp.sum(grad * x_hat, axis=0, keepdims=True), t_bias + jnp.sum(grad, axis=0, keepdims=True)
         none = jnp.zeros((1, d_model), F32)
         d_ln_s, d_ln_b = lax.fori_loop(0, imgs * CHUNK_TILES, dx_body, (none, none))
-        tick(n_sub - 1)
-        for d in OFFSETS:
-            scatter_out(dp_s, dx_hbm, dx_snd, dx_rcv, d).start()
-        local_out(dp_s, dx_hbm, loc.at[3]).start()
 
         for c in range(8):
             part = slice(c * LANES, (c + 1) * LANES)
@@ -349,6 +346,10 @@
         for d in OFFSETS:
             vec_copy(d).start()
         pltpu.make_async_copy(vbuf, vec_hbm.at[me], loc.at[4]).start()
+        tick(n_sub - 1)
+        for d in OFFSETS:
+            scatter_out(dp_s, dx_hbm, dx_snd, dx_rcv, d).start()
+        local_out(dp_s, dx_hbm, loc.at[3]).start()
 
         for t in range(DOWN_LAG):
             tick(n_sub + t)

time: 427 us -> 436 us (1.021)
  Pallas kernels: 399 us -> 408 us
    pallas_call x1, Pallas kernels: 399 us -> 408 us  [local_block(): pl.pallas_call(functools.partial(block_kernel, n_dev, special), grid=(pai...]
where the time goes in v4:
time: 436 us; the launch traced here: 435 us
  Pallas kernels  408 us (94%)
  local copies, waits for them, and re-layouts  25.7 us (6%)
    pallas_call x1, Pallas kernels, local_block(): pl.pallas_call(functools.partial(block_kernel, n_dev, special), grid=(pai...  408 us
    unnamed x10, local copies, waits for them, and re-layouts  20.2 us

profile of v4, /device:TPU:0, one launch (start us, length us, event | category | flops | bytes accessed | tf_op | source)
XLA Modules:
  0.0 435.3 jit_solution(13607770971207397294)
XLA Ops:
  0.6 0.8 constant_dynamic-slice_fusion
  1.4 0.6 pad.7.xs_ref
  2.1 0.6 pad.8.dys_ref
  2.7 408.0 %shard_map.194 = (bf16[16,64,1024]{2,1,0:T(8,128)(2,1)}, bf16[16,64,1024]{2,1,0:T(8,128)(2,1)}, f32[1024,3072]{1,0:T(8,128)}, f32[1024,1024]{1,0:T(8,128)}, f32[8,88,128]{2,1,0:T(8,128)}) custom-call(bf16[16,64,1024]{2,1,0:T(8,128)(2,1)} %x_hbm.1, bf16[16,64,1024]{2,1,0:T(8,128)(2,1)} %dy_hbm.1, bf16[2,16,1024]{2,1,0:T(8,128)(2,1)} %pad.7.xs_ref, ...), custom_call_target="tpu_custom_call" | custom-call | tf_op jit(solution)/shard_map/pallas_call | solution.py:413
  410.7 1.0 slice_reduce_fusion
  411.7 0.9 slice.57
  412.7 0.6 reshape_squeeze.7
  413.3 0.6 slice_bitcast_fusion
  413.9 0.6 slice_bitcast_fusion.1
  414.5 0.6 reshape_squeeze.6
  415.1 0.0 copy-start.1
  415.1 5.5 %copy.24 = f32[1024,1024]{1,0:T(8,128)} copy(f32[1024,1024]{0,1:T(8,128)} %bitcast.20) | data formatting | bytes 8388608
  420.6 0.0 copy-done.1
  420.6 0.0 copy-start
  420.6 1.3 copy.30
  421.9 1.0 copy-done
  423.0 1.3 copy.31
  424.3 11.0 %copy.32 = f32[1024,3072]{1,0:T(8,128)} copy(f32[1024,3072]{1,0:T(8,128)} %get-tuple-element.57) | data formatting | bytes 25165824
  (4 shorter events, 0.1 us)
Async XLA Ops:
  415.1 5.5 %copy-start.1 = (bf16[16,64,1024]{2,1,0:T(8,128)(2,1)S(1)}, bf16[16,64,1024]{2,1,0:T(8,128)(2,1)}, u32[]{:S(2)}) copy-start(bf16[16,64,1024]{2,1,0:T(8,128)(2,1)} %get-tuple-element.52) | copy-start | bytes 6291460
  420.6 2.3 copy-start
